TPU v7x, 32 devices: a whole 2x2x4 slice. The times are simulated.
32 devices in a mesh: dp: 1, ep: 32 (over x, y, z, core).
Axes of the slice: x: 2, y: 2, z: 4, core: 2. Of those that a mesh axis runs over, the one named last changes fastest.
Arguments:
- x: bfloat16 [1, 32, 256, 3584], P('dp', 'ep')
- expert: int32 [1, 32, 256, 8], P('dp', 'ep')
- slot: int32 [1, 32, 256, 8], P('dp', 'ep')
- gate: float32 [1, 32, 256, 8], P('dp', 'ep')
- w_gate: bfloat16 [64, 3584, 2048], P('ep')
- w_up: bfloat16 [64, 3584, 2048], P('ep')
- w_down: bfloat16 [64, 2048, 3584], P('ep')
- s_gate: bfloat16 [3584, 2048], replicated
- s_up: bfloat16 [3584, 2048], replicated
- s_down: bfloat16 [2048, 3584], replicated
Outputs:
- y: bfloat16 [1, 32, 256, 3584], P('dp', 'ep')
All inputs are finite; a program needn't handle non-finite values.
Results may differ from a plain program's by a relative error of at most 0.009.
Values are sent between devices in bfloat16 or wider.
A program may use at most 2 GiB of HBM per device.

v0:
```python
import jax
import jax.numpy as jnp
from jax import lax
from jax.sharding import NamedSharding, PartitionSpec as P


def einsum(form, a, b):
    return jnp.einsum(form, a.astype(jnp.float32), b.astype(jnp.float32))


def for_all(x, s_gate, s_up, s_down):
    h = jax.nn.silu(einsum("...d,df->...f", x, s_gate)) * einsum("...d,df->...f", x, s_up)
    return einsum("...f,fd->...d", h.astype(jnp.bfloat16), s_down)


def solution(mesh):
    def placed(v, *spec):
        return lax.with_sharding_constraint(v, NamedSharding(mesh, P(*spec)))

    def step(x, expert, slot, gate, w_gate, w_up, w_down, s_gate, s_up, s_down):
        experts, (tokens, top) = w_gate.shape[0], expert.shape[2:]
        slots = 5 * tokens * top // (4 * experts)
        to_expert = jax.nn.one_hot(expert, experts, dtype=jnp.bfloat16)
        to_slot = jax.nn.one_hot(slot, slots, dtype=jnp.bfloat16)
        weighted = to_expert * gate[..., None].astype(jnp.bfloat16)
        dispatch = einsum("abtke,abtkc->abtec", to_expert, to_slot).astype(jnp.bfloat16)
        combine = einsum("abtke,abtkc->abtec", weighted, to_slot).astype(jnp.bfloat16)
        z = einsum("abtec,abtd->aebcd", dispatch, x).astype(jnp.bfloat16)
        z = placed(z, "dp", None, "ep", None, None)
        z = placed(z, "dp", "ep", None, None, None)
        h = jax.nn.silu(einsum("aebcd,edf->aebcf", z, w_gate))
        h = (h * einsum("aebcd,edf->aebcf", z, w_up)).astype(jnp.bfloat16)
        out = einsum("aebcf,efd->aebcd", h, w_down).astype(jnp.bfloat16)
        out = placed(out, "dp", "ep", None, None, None)
        out = placed(out, "dp", None, "ep", None, None)
        y = einsum("abtec,aebcd->abtd", combine, out)
        return (y + for_all(x, s_gate, s_up, s_down)).astype(jnp.bfloat16)

    return step
```

profile of v0, /device:TPU:21, one launch (start us, length us, event | category | flops | bytes accessed | tf_op | source)
XLA Modules:
  0.0 1000.5 jit_solution(5115355958968056860)
XLA Ops:
  0.0 0.0 copy-start
  0.0 1.0 copy.10
  1.0 0.0 copy-start.1
  1.0 0.8 copy.12
  1.8 0.0 copy-done.1
  1.8 0.0 copy-start.3
  1.8 0.6 copy-done.3
  2.5 3.6 convolution_convert_fusion.1
  6.1 5.6 copy.13
  11.7 0.0 copy-done
  11.8 8.9 convolution_convert_fusion
  20.6 401.7 %all-to-all.4 = bf16[1,32,2,1,40,3584]{5,4,2,3,0,1:T(8,128)(2,1)} all-to-all(bf16[1,32,2,1,40,3584]{5,4,2,3,0,1:T(8,128)(2,1)} %bitcast.147), channel_id=1, replica_groups=mesh['dp'=1,'ep'=32] {'ep'}, dimensions={1} | all-to-all | bytes 36700160 | tf_op jit(solution)/sharding_constraint;jit(solution)/sharding_constraint | solution.py:18
  422.3 47.2 %fusion.2 = f32[2,32,40,2048]{3,2,1,0:T(8,128)} fusion(bf16[2,3584,2048]{2,1,0:T(8,128)(2,1)} %param.5, bf16[1,32,2,1,40,3584]{5,4,2,3,0,1:T(8,128)(2,1)} %all-to-all.4), kind=kOutput, calls=%fused_computation.2 | convolution fusion | flops 37580963840 | bytes 68681728 | tf_op jit(solution)/aebcd,edf->aebcf/dot_general | solution.py:8
  469.4 47.1 %fusion.4 = f32[2,32,40,2048]{3,2,1,0:T(8,128)} fusion(bf16[2,3584,2048]{2,1,0:T(8,128)(2,1)} %param.4, bf16[1,32,2,1,40,3584]{5,4,2,3,0,1:T(8,128)(2,1)} %all-to-all.4), kind=kOutput, calls=%fused_computation.4 | convolution fusion | flops 37580963840 | bytes 68681728 | tf_op jit(solution)/aebcd,edf->aebcf/dot_general | solution.py:8
  516.5 52.9 %convert_bitcast_fusion = bf16[1,2,32,1,40,3584]{5,4,2,1,3,0:T(8,128)(2,1)} fusion(bf16[2,2048,3584]{2,1,0:T(8,128)(2,1)} %param.6, f32[2,32,40,2048]{3,2,1,0:T(8,128)} %fusion.2, f32[2,32,40,2048]{3,2,1,0:T(8,128)} %fusion.4), kind=kOutput, calls=%fused_computation.15 | convolution fusion | flops 37621596160 | bytes 89653248 | tf_op jit(solution)/aebcf,efd->aebcd/dot_general | solution.py:8
  569.4 16.0 %copy.16 = bf16[1,2,32,1,40,3584]{5,4,1,3,0,2:T(8,128)(2,1)} copy(bf16[1,2,32,1,40,3584]{5,4,2,1,3,0:T(8,128)(2,1)} %convert_bitcast_fusion) | data formatting | bytes 36700160 | tf_op jit(solution)/sharding_constraint;jit(solution)/sharding_constraint | solution.py:18
  585.4 0.0 copy-start.5
  585.4 0.0 copy-start.2
  585.4 0.0 copy-start.4
  585.4 6.9 all-to-all-start.1
  592.3 0.0 copy-done.5
  592.3 0.1 copy.11
  592.4 0.0 copy-done.2
  592.4 0.0 copy-done.4
  592.4 4.3 convolution_convert_fusion.2
  596.7 5.6 copy.23
  602.4 8.8 convolution_bitcast_fusion.2
  611.2 19.7 %fusion.34 = f32[256,3584]{1,0:T(8,128)} fusion(bf16[2048,3584]{1,0:T(8,128)(2,1)} %param.9, bf16[3584,2048]{1,0:T(8,128)(2,1)} %param.8, f32[1,256,2048]{2,1,0:T(8,128)} %convolution_bitcast_fusion.2, bf16[1,1,256,3584]{3,2,1,0:T(8,128)(2,1)S(1)} %copy-done), kind=kOutput, calls=%fused_computation.39 | convolution fusion | flops 7519338496 | bytes 36962304 | tf_op jit(solution)/...f,fd->...d/dot_general | solution.py:8
  630.9 356.7 %all-to-all-done.1 = bf16[1,2,32,1,40,3584]{5,4,1,3,0,2:T(8,128)(2,1)} async-done(((bf16[1,2,32,1,40,3584]{5,4,1,3,0,2:T(8,128)(2,1)}), bf16[1,2,32,1,40,3584]{5,4,1,3,0,2:T(8,128)(2,1)}, u32[]{:S(2)}, u32[]{:S(2)}) %all-to-all-start.1) | async-done | bytes 18350112 | tf_op jit(solution)/sharding_constraint;jit(solution)/sharding_constraint | solution.py:18
  987.6 12.9 %fusion.20 = bf16[1,1,256,3584]{3,2,1,0:T(8,128)(2,1)} fusion(f32[256,3584]{1,0:T(8,128)} %fusion.34, bf16[256,64,40]{0,2,1:T(8,128)(2,1)S(1)} %copy.23, bf16[64,40,3584]{2,1,0:T(8,128)(2,1)} %bitcast.38), kind=kOutput, calls=%fused_computation.23 | convolution fusion | flops 4699455488 | bytes 25165824 | tf_op jit(solution)/abtec,aebcd->abtd/dot_general | solution.py:8
  (1 shorter events, 0.0 us)
Async XLA Ops:
  0.0 11.7 %copy-start = (bf16[1,1,256,3584]{3,2,1,0:T(8,128)(2,1)S(1)}, bf16[1,1,256,3584]{3,2,1,0:T(8,128)(2,1)}, u32[]{:S(2)}) copy-start(bf16[1,1,256,3584]{3,2,1,0:T(8,128)(2,1)} %param.3) | copy-start | bytes 5505028
  1.0 0.9 copy-start.1
  1.8 0.7 copy-start.3
  585.4 6.9 copy-start.5
  585.4 7.0 copy-start.2
  585.4 7.0 copy-start.4
  585.4 402.2 %all-to-all-start.1 = ((bf16[1,2,32,1,40,3584]{5,4,1,3,0,2:T(8,128)(2,1)}), bf16[1,2,32,1,40,3584]{5,4,1,3,0,2:T(8,128)(2,1)}, u32[]{:S(2)}, u32[]{:S(2)}) async-start(bf16[1,2,32,1,40,3584]{5,4,1,3,0,2:T(8,128)(2,1)} %copy.16), calls=%async_computation.1 | async-start | bytes 36700160 | tf_op jit(solution)/sharding_constraint;jit(solution)/sharding_constraint | solution.py:18
where the time goes:
time: 1010 us; the launch traced here: 1000 us
  blocking collectives  402 us (40%)
  waiting for transfers between devices  357 us (35%)
  matrix products  205 us (20%)
  local copies, waits for them, and re-layouts  29.8 us (3%)
    another operation x1, blocking collectives, placed(): return lax.with_sharding_constraint(v, NamedSharding(mesh, P(*spec)))  402 us
    another operation x1, waiting for transfers between devices, placed(): return lax.with_sharding_constraint(v, NamedSharding(mesh, P(*spec)))  357 us
    dot_general x9, matrix products, einsum(): return jnp.einsum(form, a.astype(jnp.float32), b.astype(jnp.float32))  205 us
  transfers between devices with their start and end apart: 1, of which 1 were waited for; matrix products, arithmetic and copies ran while one was open for 4% of the time, Pallas kernels for 0%

commit v1 on v0

v1 whole, which is shorter than its diff:
```python
import jax
import jax.numpy as jnp
from jax import lax
from jax.sharding import PartitionSpec as P


BF16, F32 = jnp.bfloat16, jnp.float32


def dot(a, b):
    return jnp.dot(a, b, preferred_element_type=F32)


def after(v, *earlier):
    return lax.optimization_barrier((v, *earlier))[0]


def solution(mesh):
    n = mesh.shape["ep"]

    def swap(v, mask):
        return lax.ppermute(v, "ep", [(a, a ^ mask) for a in range(n)])

    def layer(x, expert, slot, gate, w_gate, w_up, w_down, s_gate, s_up, s_down):
        x, expert, slot, gate = x[0, 0], expert[0, 0], slot[0, 0], gate[0, 0]
        tokens, width = x.shape
        top = expert.shape[1]
        per = w_gate.shape[0]
        slots = 5 * tokens * top // (4 * per * n)
        me = lax.axis_index("ep")
        column = [[c * 8 + i for i in range(8)] for c in range(n // 8)]
        place = jnp.where(slot < slots, expert * slots + slot, -1).astype(F32)
        info = jnp.stack([place, gate.astype(BF16).astype(F32)])
        info = lax.all_gather(info, "ep", axis_index_groups=column)
        here = me % 8
        far = after(x, info)
        from_z = {g: swap(far, g << 1) if g else x for g in range(4)}

        def routes(g):
            pieces = [lax.dynamic_index_in_dim(info, here ^ (2 * g + r), 0, False) for r in range(2)]
            return [p[0].astype(jnp.int32) for p in pieces], [p[1] for p in pieces]

        rows = 4 * per * 2 * slots
        row = lax.iota(jnp.int32, rows)
        c, r, e, i = row % slots, row // slots % 2, row // (2 * slots) % per, row // (2 * slots * per)
        wanted = ((me ^ (i << 3)) * per + e) * slots + c
        block = per * 2 * slots

        def pick(g, last):
            near = after(from_z[g], *last) if last else from_z[g]
            both = jnp.concatenate([near, swap(near, 1)])
            places, _ = routes(g)
            halves = []
            for q in range(2):
                hit = (r == q)[:, None] & (places[q][:, 0][None, :] == wanted[:, None])
                for j in range(1, top):
                    hit = hit | ((r == q)[:, None] & (places[q][:, j][None, :] == wanted[:, None]))
                halves.append(hit.astype(BF16))
            chosen = jnp.concatenate(halves, axis=1)
            return dot(chosen, both).astype(BF16)

        def send(z):
            cut = [z[k * block:(k + 1) * block] for k in range(4)]
            return cut[:1] + [swap(cut[k], k << 3) for k in range(1, 4)], cut[1:]

        def ffn(parts, last):
            z = jnp.stack(parts).reshape(4, per, 2 * slots, width)
            z = z.transpose(1, 0, 2, 3).reshape(per, 8 * slots, width)
            z = after(z, *last)
            h = jax.nn.silu(jnp.einsum("ebd,edf->ebf", z, w_gate, preferred_element_type=F32))
            h = (h * jnp.einsum("ebd,edf->ebf", z, w_up, preferred_element_type=F32)).astype(BF16)
            return jnp.einsum("ebf,efd->ebd", h, w_down, preferred_element_type=F32).astype(BF16)

        def cuts(out):
            out = out.reshape(per, 4, 2 * slots, width)
            return [out[:, k].reshape(block, width) for k in range(4)]

        def reply(cut):
            return cut[:1] + [swap(cut[k], k << 3) for k in range(1, 4)]

        def combine(g, back, last):
            _, gates = routes(g)
            places, _ = routes(g)
            halves = []
            for q in range(2):
                w = jnp.zeros((tokens, rows), F32)
                for j in range(top):
                    t = (places[q][:, j][:, None] == wanted[None, :]) & (r == q)[None, :]
                    w = jnp.where(t, gates[q][:, j][:, None], w)
                halves.append(w.astype(BF16))
            weigh = jnp.concatenate(halves, axis=0)
            if last:
                weigh = after(weigh, *last)
            both = dot(weigh, jnp.concatenate(back))
            own = both[:tokens] + swap(both[tokens:].astype(BF16), 1).astype(F32)
            return own if g == 0 else swap(own.astype(BF16), g << 1)

        def shared(xs):
            h = jax.nn.silu(dot(xs, s_gate)) * dot(xs, s_up)
            return dot(h.astype(BF16), s_down)

        d0, t0 = send(pick(0, []))
        total = shared(after(x, *t0))
        d1, t1 = send(pick(1, [total]))
        o0 = cuts(ffn(d0, t1))
        b0 = reply(o0)
        d3, t3 = send(pick(3, o0))
        o1 = cuts(ffn(d1, t3))
        b1 = reply(o1)
        d2, t2 = send(pick(2, o1))
        o3 = cuts(ffn(d3, t2))
        b3 = reply(o3)
        p0 = combine(0, b0, o3)
        o2 = cuts(ffn(d2, [p0]))
        b2 = reply(o2)
        p1 = combine(1, b1, o2)
        p3 = combine(3, b3, [p1])
        p2 = combine(2, b2, [p3])
        total = total + p0 + p3.astype(F32)
        total = total + p2.astype(F32) + p1.astype(F32)
        return total.astype(BF16)[None, None]

    token = P("dp", "ep", None, None)
    weight = P("ep", None, None)

    return jax.shard_map(
        layer,
        mesh=mesh,
        in_specs=(token,) * 4 + (weight,) * 3 + (P(None, None),) * 3,
        out_specs=token,
        check_vma=False,
    )
```

time: 1010 us -> 780 us (0.77)
  blocking collectives: 402 us -> 12.1 us
  matrix products: 205 us -> 267 us
  waiting for transfers between devices: 357 us -> 391 us
  other arithmetic: 0.01 us -> 32.7 us
  starting transfers between devices: 6.86 us -> 38.5 us
    another operation x1 -> x0, blocking collectives: 402 us -> none  [placed(): return lax.with_sharding_constraint(v, NamedSharding(mesh, P(*spec)))]
    ppermute x0 -> x38, waiting for transfers between devices: none -> 391 us  [swap(): return lax.ppermute(v, 'ep', [(a, a ^ mask) for a in range(n)])]
    another operation x1 -> x0, waiting for transfers between devices: 357 us -> none  [placed(): return lax.with_sharding_constraint(v, NamedSharding(mesh, P(*spec)))]
    dot_general x9 -> x18, matrix products: 205 us -> 267 us  [the longest x4 133 us: ffn(): jnp.einsum('ebf,efd->ebd', h, w_down, preferred_element_type=F32)]
    ppermute x0 -> x38, starting transfers between devices: none -> 38.5 us  [swap(): return lax.ppermute(v, 'ep', [(a, a ^ mask) for a in range(n)])]
    slice x0 -> x20, local copies, waits for them, and re-layouts: none -> 23.4 us  [the longest x4 16.2 us: cuts(): return [out[:, k].reshape(block, width) for k in range(4)]]
    another operation x1 -> x0, local copies, waits for them, and re-layouts: 16 us -> none  [placed(): return lax.with_sharding_constraint(v, NamedSharding(mesh, P(*spec)))]
    convert_element_type x1 -> x13, other arithmetic: 0.01 us -> 12.2 us  [the longest x8 9.3 us: combine(): halves.append(w.astype(BF16))]
  transfers between devices with their start and end apart: 1 -> 38, of which waited for: 1 -> 16; matrix products, arithmetic and copies ran while one was open for 4% -> 39% of each run, Pallas kernels for 0% -> 0%
where the time goes in v1:
time: 780 us; the launch traced here: 772 us
  waiting for transfers between devices  391 us (50%)
  matrix products  267 us (34%)
  starting transfers between devices  38.5 us (5%)
  other arithmetic  32.7 us (4%)
  local copies, waits for them, and re-layouts  27.9 us (4%)
  blocking collectives  12.1 us (2%)
    ppermute x38, waiting for transfers between devices, swap(): return lax.ppermute(v, 'ep', [(a, a ^ mask) for a in range(n)])  391 us
    dot_general x4, matrix products, ffn(): jnp.einsum('ebf,efd->ebd', h, w_down, preferred_element_type=F32)  133 us
    dot_general x4, matrix products, ffn(): jnp.einsum('ebd,edf->ebf', z, w_gate, preferred_element_type=F32)  70.9 us
    dot_general x10, matrix products, dot(): return jnp.dot(a, b, preferred_element_type=F32)  63 us
    ppermute x38, starting transfers between devices, swap(): return lax.ppermute(v, 'ep', [(a, a ^ mask) for a in range(n)])  38.5 us
    slice x4, local copies, waits for them, and re-layouts, cuts(): return [out[:, k].reshape(block, width) for k in range(4)]  16.2 us
  transfers between devices with their start and end apart: 38, of which 16 were waited for; matrix products, arithmetic and copies ran while one was open for 39% of the time, Pallas kernels for 0%

profile of v1, /device:TPU:21, one launch (start us, length us, event | category | flops | bytes accessed | tf_op | source)
XLA Modules:
  0.0 772.1 jit_solution(14441876179449890040)
XLA Ops:
  2.1 12.1 %all-gather = f32[16,256,8]{1,2,0:T(8,128)S(1)} all-gather(f32[2,256,8]{1,2,0:T(8,128)S(1)} %pad_maximum_fusion.4), channel_id=2, replica_groups={{0,1,2,3,4,5,6,7},{8,9,10,11,12,13,14,15},{16,17,18,19,20,21,22,23},{24..., dimensions={0}, use_global_device_ids=true | all-gather | bytes 147456 | tf_op jit(solution)/shard_map/all_gather | solution.py:34
  23.8 4.2 convolution_convert_fusion.7
  30.0 6.7 fusion.126
  36.7 20.2 %fusion.61 = f32[256,3584]{1,0:T(8,128)} fusion(bf16[2048,3584]{1,0:T(8,128)(2,1)} %param.19, bf16[256,3584]{1,0:T(8,128)(2,1)} %bitcast, bf16[3584,2048]{1,0:T(8,128)(2,1)} %param.18, f32[256,2048]{1,0:T(8,128)} %fusion.126), kind=kOutput, calls=%fused_computation.87 | convolution fusion | flops 7519338496 | bytes 36962304 | tf_op jit(solution)/shard_map/dot_general | solution.py:11
  61.7 23.9 %collective-permute-done.2 = bf16[160,3584]{1,0:T(8,128)(2,1)S(1)} collective-permute-done((bf16[160,3584]{1,0:T(8,128)(2,1)}, bf16[160,3584]{1,0:T(8,128)(2,1)S(1)}, u32[]{:S(2)}, u32[]{:S(2)}) %collective-permute-start.2) | collective-permute-done | bytes 1146912 | tf_op jit(solution)/shard_map/ppermute | solution.py:22
  85.6 25.2 %collective-permute-done.4 = bf16[160,3584]{1,0:T(8,128)(2,1)S(1)} collective-permute-done((bf16[160,3584]{1,0:T(8,128)(2,1)S(1)}, bf16[160,3584]{1,0:T(8,128)(2,1)S(1)}, u32[]{:S(2)}, u32[]{:S(2)}) %collective-permute-start.4) | collective-permute-done | bytes 1146912 | tf_op jit(solution)/shard_map/ppermute | solution.py:22
  112.6 5.0 convolution_convert_fusion.6
  118.9 17.8 %fusion.127 = f32[2,320,2048]{2,1,0:T(8,128)} fusion(bf16[2,320,3584]{2,1,0:T(8,128)(2,1)S(1)} %bitcast.286, bf16[2,3584,2048]{2,1,0:T(8,128)(2,1)} %param.14), kind=kOutput, calls=%fused_computation.210 | convolution fusion | flops 9395240960 | bytes 39190528 | tf_op jit(solution)/shard_map/ebd,edf->ebf/dot_general | solution.py:70
  136.7 33.5 %convolution_convert_fusion.5 = bf16[2,320,3584]{2,1,0:T(8,128)(2,1)} fusion(bf16[2,2048,3584]{2,1,0:T(8,128)(2,1)} %param.16, f32[2,320,2048]{2,1,0:T(8,128)} %fusion.127, bf16[2,320,3584]{2,1,0:T(8,128)(2,1)} %bitcast.287, bf16[2,3584,2048]{2,1,0:T(8,128)(2,1)} %param.15), kind=kOutput, calls=%fused_computation.5 | convolution fusion | flops 18800640000 | bytes 73138176 | tf_op jit(solution)/shard_map/ebf,efd->ebd/dot_general | solution.py:72
  170.2 4.6 fusion.107
  184.4 18.6 %collective-permute-done.12 = bf16[160,3584]{1,0:T(8,128)(2,1)S(1)} collective-permute-done((bf16[160,3584]{1,0:T(8,128)(2,1)S(1)}, bf16[160,3584]{1,0:T(8,128)(2,1)S(1)}, u32[]{:S(2)}, u32[]{:S(2)}) %collective-permute-start.12) | collective-permute-done | bytes 1146912 | tf_op jit(solution)/shard_map/ppermute | solution.py:22
  203.0 25.4 %collective-permute-done.14 = bf16[160,3584]{1,0:T(8,128)(2,1)S(1)} collective-permute-done((bf16[160,3584]{1,0:T(8,128)(2,1)S(1)}, bf16[160,3584]{1,0:T(8,128)(2,1)S(1)}, u32[]{:S(2)}, u32[]{:S(2)}) %collective-permute-start.14) | collective-permute-done | bytes 1146912 | tf_op jit(solution)/shard_map/ppermute | solution.py:22
  229.6 5.4 convolution_convert_fusion.4
  236.9 17.7 %fusion.128 = f32[2,320,2048]{2,1,0:T(8,128)} fusion(bf16[2,320,3584]{2,1,0:T(8,128)(2,1)S(1)} %bitcast.290, bf16[2,3584,2048]{2,1,0:T(8,128)(2,1)} %param.14), kind=kOutput, calls=%fused_computation.211 | convolution fusion | flops 9395240960 | bytes 39190528 | tf_op jit(solution)/shard_map/ebd,edf->ebf/dot_general | solution.py:70
  254.6 33.2 %convolution_convert_fusion.3 = bf16[2,320,3584]{2,1,0:T(8,128)(2,1)} fusion(bf16[2,2048,3584]{2,1,0:T(8,128)(2,1)} %param.16, f32[2,320,2048]{2,1,0:T(8,128)} %fusion.128, bf16[2,320,3584]{2,1,0:T(8,128)(2,1)} %bitcast.291, bf16[2,3584,2048]{2,1,0:T(8,128)(2,1)} %param.15), kind=kOutput, calls=%fused_computation.3 | convolution fusion | flops 18800640000 | bytes 73138176 | tf_op jit(solution)/shard_map/ebf,efd->ebd/dot_general | solution.py:72
  288.0 4.3 fusion.106
  300.4 20.1 %collective-permute-done.8 = bf16[160,3584]{1,0:T(8,128)(2,1)S(1)} collective-permute-done((bf16[160,3584]{1,0:T(8,128)(2,1)S(1)}, bf16[160,3584]{1,0:T(8,128)(2,1)S(1)}, u32[]{:S(2)}, u32[]{:S(2)}) %collective-permute-start.8) | collective-permute-done | bytes 1146912 | tf_op jit(solution)/shard_map/ppermute | solution.py:22
  322.7 23.4 %collective-permute-done.10 = bf16[160,3584]{1,0:T(8,128)(2,1)S(1)} collective-permute-done((bf16[160,3584]{1,0:T(8,128)(2,1)S(1)}, bf16[160,3584]{1,0:T(8,128)(2,1)S(1)}, u32[]{:S(2)}, u32[]{:S(2)}) %collective-permute-start.10) | collective-permute-done | bytes 1146912 | tf_op jit(solution)/shard_map/ppermute | solution.py:22
  347.7 5.0 convolution_convert_fusion.2
  354.6 17.7 %fusion.129 = f32[2,320,2048]{2,1,0:T(8,128)} fusion(bf16[2,320,3584]{2,1,0:T(8,128)(2,1)S(1)} %bitcast.288, bf16[2,3584,2048]{2,1,0:T(8,128)(2,1)} %param.14), kind=kOutput, calls=%fused_computation.212 | convolution fusion | flops 9395240960 | bytes 39190528 | tf_op jit(solution)/shard_map/ebd,edf->ebf/dot_general | solution.py:70
  372.3 33.2 %convolution_convert_fusion.1 = bf16[2,320,3584]{2,1,0:T(8,128)(2,1)} fusion(bf16[2,2048,3584]{2,1,0:T(8,128)(2,1)} %param.16, f32[2,320,2048]{2,1,0:T(8,128)} %fusion.129, bf16[2,320,3584]{2,1,0:T(8,128)(2,1)} %bitcast.289, bf16[2,3584,2048]{2,1,0:T(8,128)(2,1)} %param.15), kind=kOutput, calls=%fused_computation.1 | convolution fusion | flops 18800640000 | bytes 73138176 | tf_op jit(solution)/shard_map/ebf,efd->ebd/dot_general | solution.py:72
  405.4 4.6 fusion.103
  410.3 5.1 fusion
  423.9 20.5 %collective-permute-done.20 = bf16[160,3584]{1,0:T(8,128)(2,1)S(1)} collective-permute-done((bf16[160,3584]{1,0:T(8,128)(2,1)S(1)}, bf16[160,3584]{1,0:T(8,128)(2,1)S(1)}, u32[]{:S(2)}, u32[]{:S(2)}) %collective-permute-start.20) | collective-permute-done | bytes 1146912 | tf_op jit(solution)/shard_map/ppermute | solution.py:22
  446.5 23.4 %collective-permute-done.22 = bf16[160,3584]{1,0:T(8,128)(2,1)S(1)} collective-permute-done((bf16[160,3584]{1,0:T(8,128)(2,1)S(1)}, bf16[160,3584]{1,0:T(8,128)(2,1)S(1)}, u32[]{:S(2)}, u32[]{:S(2)}) %collective-permute-start.22) | collective-permute-done | bytes 1146912 | tf_op jit(solution)/shard_map/ppermute | solution.py:22
  474.2 17.8 %fusion.130 = f32[2,320,2048]{2,1,0:T(8,128)} fusion(bf16[2,320,3584]{2,1,0:T(8,128)(2,1)S(1)} %bitcast.292, bf16[2,3584,2048]{2,1,0:T(8,128)(2,1)} %param.14), kind=kOutput, calls=%fused_computation.213 | convolution fusion | flops 9395240960 | bytes 39190528 | tf_op jit(solution)/shard_map/ebd,edf->ebf/dot_general | solution.py:70
  492.0 33.1 %convolution_convert_fusion = bf16[2,320,3584]{2,1,0:T(8,128)(2,1)} fusion(bf16[2,2048,3584]{2,1,0:T(8,128)(2,1)} %param.16, f32[2,320,2048]{2,1,0:T(8,128)} %fusion.130, bf16[2,320,3584]{2,1,0:T(8,128)(2,1)} %bitcast.293, bf16[2,3584,2048]{2,1,0:T(8,128)(2,1)} %param.15), kind=kOutput, calls=%fused_computation | convolution fusion | flops 18800640000 | bytes 73138176 | tf_op jit(solution)/shard_map/ebf,efd->ebd/dot_general | solution.py:72
  527.8 4.9 fusion.8
  545.6 34.8 %collective-permute-done.27 = bf16[256,3584]{1,0:T(8,128)(2,1)S(1)} collective-permute-done((bf16[256,3584]{1,0:T(8,128)(2,1)S(1)}, bf16[256,3584]{1,0:T(8,128)(2,1)S(1)}, u32[]{:S(2)}, u32[]{:S(2)}) %collective-permute-start.27) | collective-permute-done | bytes 1835040 | tf_op jit(solution)/shard_map/ppermute | solution.py:22
  580.5 11.7 %collective-permute-done.30 = bf16[160,3584]{1,0:T(8,128)(2,1)S(1)} collective-permute-done((bf16[160,3584]{1,0:T(8,128)(2,1)S(1)}, bf16[160,3584]{1,0:T(8,128)(2,1)S(1)}, u32[]{:S(2)}, u32[]{:S(2)}) %collective-permute-start.30) | collective-permute-done | bytes 1146912 | tf_op jit(solution)/shard_map/ppermute | solution.py:22
  607.7 74.4 %collective-permute-done.32 = bf16[256,3584]{1,0:T(8,128)(2,1)S(1)} collective-permute-done((bf16[256,3584]{1,0:T(8,128)(2,1)S(1)}, bf16[256,3584]{1,0:T(8,128)(2,1)S(1)}, u32[]{:S(2)}, u32[]{:S(2)}) %collective-permute-start.32) | collective-permute-done | bytes 1835040 | tf_op jit(solution)/shard_map/ppermute | solution.py:22
  690.9 78.6 %collective-permute-done.37 = bf16[256,3584]{1,0:T(8,128)(2,1)S(1)} collective-permute-done((bf16[256,3584]{1,0:T(8,128)(2,1)S(1)}, bf16[256,3584]{1,0:T(8,128)(2,1)S(1)}, u32[]{:S(2)}, u32[]{:S(2)}) %collective-permute-start.37) | collective-permute-done | bytes 1835040 | tf_op jit(solution)/shard_map/ppermute | solution.py:22
  (440 shorter events, 103.1 us)
Async XLA Ops:
  14.2 43.6 %collective-permute-start.5 = (bf16[256,3584]{1,0:T(8,128)(2,1)}, bf16[256,3584]{1,0:T(8,128)(2,1)}, u32[]{:S(2)}, u32[]{:S(2)}) collective-permute-start(bf16[256,3584]{1,0:T(8,128)(2,1)} %bitcast), channel_id=1, source_target_pairs={{0,2},{1,3},{2,0},{3,1},{4,6},{5,7},{6,4},{7,5},{8,10},{9,11},{10,... | collective-permute-start | bytes 5505032 | tf_op jit(solution)/shard_map/ppermute | solution.py:22
  57.7 54.2 %collective-permute-start.6 = (bf16[256,3584]{1,0:T(8,128)(2,1)}, bf16[256,3584]{1,0:T(8,128)(2,1)S(1)}, u32[]{:S(2)}, u32[]{:S(2)}) collective-permute-start(bf16[256,3584]{1,0:T(8,128)(2,1)} %collective-permute-done.5), channel_id=1, source_target_pairs={{0,1},{1,0},{2,3},{3,2},{4,5},{5,4},{6,7},{7,6},{8,9},{9,8},{10,11... | collective-permute-start | bytes 5505032 | tf_op jit(solution)/shard_map/ppermute | solution.py:22
  58.5 27.1 %collective-permute-start.2 = (bf16[160,3584]{1,0:T(8,128)(2,1)}, bf16[160,3584]{1,0:T(8,128)(2,1)S(1)}, u32[]{:S(2)}, u32[]{:S(2)}) collective-permute-start(bf16[160,3584]{1,0:T(8,128)(2,1)} %get-tuple-element.58), channel_id=1, source_target_pairs={{0,8},{1,9},{2,10},{3,11},{4,12},{5,13},{6,14},{7,15},{8,0},{9,1},... | collective-permute-start | bytes 3440648 | tf_op jit(solution)/shard_map/ppermute | solution.py:22
  58.7 26.9 %collective-permute-start.3 = (bf16[160,3584]{1,0:T(8,128)(2,1)S(1)}, bf16[160,3584]{1,0:T(8,128)(2,1)S(1)}, u32[]{:S(2)}, u32[]{:S(2)}) collective-permute-start(bf16[160,3584]{1,0:T(8,128)(2,1)S(1)} %get-tuple-element.57), channel_id=1, source_target_pairs={{0,16},{1,17},{2,18},{3,19},{4,20},{5,21},{6,22},{7,23},{8,24},{9,... | collective-permute-start | bytes 3440648 | tf_op jit(solution)/shard_map/ppermute | solution.py:22
  59.9 50.9 %collective-permute-start.4 = (bf16[160,3584]{1,0:T(8,128)(2,1)S(1)}, bf16[160,3584]{1,0:T(8,128)(2,1)S(1)}, u32[]{:S(2)}, u32[]{:S(2)}) collective-permute-start(bf16[160,3584]{1,0:T(8,128)(2,1)S(1)} %get-tuple-element.56), channel_id=1, source_target_pairs={{0,24},{1,25},{2,26},{3,27},{4,28},{5,29},{6,30},{7,31},{8,16},{9,... | collective-permute-start | bytes 3440648 | tf_op jit(solution)/shard_map/ppermute | solution.py:22
  61.1 113.6 %collective-permute-start.1 = (bf16[256,3584]{1,0:T(8,128)(2,1)}, bf16[256,3584]{1,0:T(8,128)(2,1)}, u32[]{:S(2)}, u32[]{:S(2)}) collective-permute-start(bf16[256,3584]{1,0:T(8,128)(2,1)} %bitcast), channel_id=1, source_target_pairs={{0,6},{1,7},{2,4},{3,5},{4,2},{5,3},{6,0},{7,1},{8,14},{9,15},{10,... | collective-permute-start | bytes 5505032 | tf_op jit(solution)/shard_map/ppermute | solution.py:22
  174.8 54.8 %collective-permute-start.7 = (bf16[256,3584]{1,0:T(8,128)(2,1)}, bf16[256,3584]{1,0:T(8,128)(2,1)S(1)}, u32[]{:S(2)}, u32[]{:S(2)}) collective-permute-start(bf16[256,3584]{1,0:T(8,128)(2,1)} %collective-permute-done.1), channel_id=1, source_target_pairs={{0,1},{1,0},{2,3},{3,2},{4,5},{5,4},{6,7},{7,6},{8,9},{9,8},{10,11... | collective-permute-start | bytes 5505032 | tf_op jit(solution)/shard_map/ppermute | solution.py:22
  175.9 116.4 %collective-permute-start.11 = (bf16[256,3584]{1,0:T(8,128)(2,1)}, bf16[256,3584]{1,0:T(8,128)(2,1)}, u32[]{:S(2)}, u32[]{:S(2)}) collective-permute-start(bf16[256,3584]{1,0:T(8,128)(2,1)} %bitcast), channel_id=1, source_target_pairs={{0,4},{1,5},{2,6},{3,7},{4,0},{5,1},{6,2},{7,3},{8,12},{9,13},{10,... | collective-permute-start | bytes 5505032 | tf_op jit(solution)/shard_map/ppermute | solution.py:22
  177.8 50.5 %collective-permute-start.14 = (bf16[160,3584]{1,0:T(8,128)(2,1)S(1)}, bf16[160,3584]{1,0:T(8,128)(2,1)S(1)}, u32[]{:S(2)}, u32[]{:S(2)}) collective-permute-start(bf16[160,3584]{1,0:T(8,128)(2,1)S(1)} %get-tuple-element.60), channel_id=1, source_target_pairs={{0,24},{1,25},{2,26},{3,27},{4,28},{5,29},{6,30},{7,31},{8,16},{9,... | collective-permute-start | bytes 3440648 | tf_op jit(solution)/shard_map/ppermute | solution.py:22
  292.3 54.7 %collective-permute-start.15 = (bf16[256,3584]{1,0:T(8,128)(2,1)}, bf16[256,3584]{1,0:T(8,128)(2,1)S(1)}, u32[]{:S(2)}, u32[]{:S(2)}) collective-permute-start(bf16[256,3584]{1,0:T(8,128)(2,1)} %collective-permute-done.11), channel_id=1, source_target_pairs={{0,1},{1,0},{2,3},{3,2},{4,5},{5,4},{6,7},{7,6},{8,9},{9,8},{10,11... | collective-permute-start | bytes 5505032 | tf_op jit(solution)/shard_map/ppermute | solution.py:22
  293.8 26.7 %collective-permute-start.8 = (bf16[160,3584]{1,0:T(8,128)(2,1)S(1)}, bf16[160,3584]{1,0:T(8,128)(2,1)S(1)}, u32[]{:S(2)}, u32[]{:S(2)}) collective-permute-start(bf16[160,3584]{1,0:T(8,128)(2,1)S(1)} %copy-done.16), channel_id=1, source_target_pairs={{0,8},{1,9},{2,10},{3,11},{4,12},{5,13},{6,14},{7,15},{8,0},{9,1},... | collective-permute-start | bytes 3440648 | tf_op jit(solution)/shard_map/ppermute | solution.py:22
  294.0 27.7 %collective-permute-start.9 = (bf16[160,3584]{1,0:T(8,128)(2,1)S(1)}, bf16[160,3584]{1,0:T(8,128)(2,1)S(1)}, u32[]{:S(2)}, u32[]{:S(2)}) collective-permute-start(bf16[160,3584]{1,0:T(8,128)(2,1)S(1)} %copy-done.15), channel_id=1, source_target_pairs={{0,16},{1,17},{2,18},{3,19},{4,20},{5,21},{6,22},{7,23},{8,24},{9,... | collective-permute-start | bytes 3440648 | tf_op jit(solution)/shard_map/ppermute | solution.py:22
  295.2 50.8 %collective-permute-start.10 = (bf16[160,3584]{1,0:T(8,128)(2,1)S(1)}, bf16[160,3584]{1,0:T(8,128)(2,1)S(1)}, u32[]{:S(2)}, u32[]{:S(2)}) collective-permute-start(bf16[160,3584]{1,0:T(8,128)(2,1)S(1)} %copy-done.14), channel_id=1, source_target_pairs={{0,24},{1,25},{2,26},{3,27},{4,28},{5,29},{6,30},{7,31},{8,16},{9,... | collective-permute-start | bytes 3440648 | tf_op jit(solution)/shard_map/ppermute | solution.py:22
  300.2 110.1 %collective-permute-start.16 = (bf16[160,3584]{1,0:T(8,128)(2,1)}, bf16[160,3584]{1,0:T(8,128)(2,1)}, u32[]{:S(2)}, u32[]{:S(2)}) collective-permute-start(bf16[160,3584]{1,0:T(8,128)(2,1)} %bitcast.84), channel_id=1, source_target_pairs={{0,8},{1,9},{2,10},{3,11},{4,12},{5,13},{6,14},{7,15},{8,0},{9,1},... | collective-permute-start | bytes 3440648 | tf_op jit(solution)/shard_map/ppermute | solution.py:22
  320.6 89.7 %collective-permute-start.17 = (bf16[160,3584]{1,0:T(8,128)(2,1)}, bf16[160,3584]{1,0:T(8,128)(2,1)}, u32[]{:S(2)}, u32[]{:S(2)}) collective-permute-start(bf16[160,3584]{1,0:T(8,128)(2,1)} %bitcast.85), channel_id=1, source_target_pairs={{0,16},{1,17},{2,18},{3,19},{4,20},{5,21},{6,22},{7,23},{8,24},{9,... | collective-permute-start | bytes 3440648 | tf_op jit(solution)/shard_map/ppermute | solution.py:22
  321.8 88.5 %collective-permute-start.18 = (bf16[160,3584]{1,0:T(8,128)(2,1)}, bf16[160,3584]{1,0:T(8,128)(2,1)}, u32[]{:S(2)}, u32[]{:S(2)}) collective-permute-start(bf16[160,3584]{1,0:T(8,128)(2,1)} %bitcast.86), channel_id=1, source_target_pairs={{0,24},{1,25},{2,26},{3,27},{4,28},{5,29},{6,30},{7,31},{8,16},{9,... | collective-permute-start | bytes 3440648 | tf_op jit(solution)/shard_map/ppermute | solution.py:22
  415.6 55.3 %collective-permute-start.19 = (bf16[256,3584]{1,0:T(8,128)(2,1)S(1)}, bf16[256,3584]{1,0:T(8,128)(2,1)S(1)}, u32[]{:S(2)}, u32[]{:S(2)}) collective-permute-start(bf16[256,3584]{1,0:T(8,128)(2,1)S(1)} %slice.1013), channel_id=1, source_target_pairs={{0,1},{1,0},{2,3},{3,2},{4,5},{5,4},{6,7},{7,6},{8,9},{9,8},{10,11... | collective-permute-start | bytes 5505032 | tf_op jit(solution)/shard_map/ppermute | solution.py:22
  417.7 26.7 %collective-permute-start.20 = (bf16[160,3584]{1,0:T(8,128)(2,1)S(1)}, bf16[160,3584]{1,0:T(8,128)(2,1)S(1)}, u32[]{:S(2)}, u32[]{:S(2)}) collective-permute-start(bf16[160,3584]{1,0:T(8,128)(2,1)S(1)} %copy-done.13), channel_id=1, source_target_pairs={{0,8},{1,9},{2,10},{3,11},{4,12},{5,13},{6,14},{7,15},{8,0},{9,1},... | collective-permute-start | bytes 3440648 | tf_op jit(solution)/shard_map/ppermute | solution.py:22
  417.9 27.7 %collective-permute-start.21 = (bf16[160,3584]{1,0:T(8,128)(2,1)S(1)}, bf16[160,3584]{1,0:T(8,128)(2,1)S(1)}, u32[]{:S(2)}, u32[]{:S(2)}) collective-permute-start(bf16[160,3584]{1,0:T(8,128)(2,1)S(1)} %copy-done.12), channel_id=1, source_target_pairs={{0,16},{1,17},{2,18},{3,19},{4,20},{5,21},{6,22},{7,23},{8,24},{9,... | collective-permute-start | bytes 3440648 | tf_op jit(solution)/shard_map/ppermute | solution.py:22
  419.1 50.8 %collective-permute-start.22 = (bf16[160,3584]{1,0:T(8,128)(2,1)S(1)}, bf16[160,3584]{1,0:T(8,128)(2,1)S(1)}, u32[]{:S(2)}, u32[]{:S(2)}) collective-permute-start(bf16[160,3584]{1,0:T(8,128)(2,1)S(1)} %copy-done.11), channel_id=1, source_target_pairs={{0,24},{1,25},{2,26},{3,27},{4,28},{5,29},{6,30},{7,31},{8,16},{9,... | collective-permute-start | bytes 3440648 | tf_op jit(solution)/shard_map/ppermute | solution.py:22
  423.7 104.1 %collective-permute-start.23 = (bf16[160,3584]{1,0:T(8,128)(2,1)}, bf16[160,3584]{1,0:T(8,128)(2,1)}, u32[]{:S(2)}, u32[]{:S(2)}) collective-permute-start(bf16[160,3584]{1,0:T(8,128)(2,1)} %bitcast.119), channel_id=1, source_target_pairs={{0,8},{1,9},{2,10},{3,11},{4,12},{5,13},{6,14},{7,15},{8,0},{9,1},... | collective-permute-start | bytes 3440648 | tf_op jit(solution)/shard_map/ppermute | solution.py:22
  444.4 83.4 %collective-permute-start.24 = (bf16[160,3584]{1,0:T(8,128)(2,1)}, bf16[160,3584]{1,0:T(8,128)(2,1)}, u32[]{:S(2)}, u32[]{:S(2)}) collective-permute-start(bf16[160,3584]{1,0:T(8,128)(2,1)} %bitcast.120), channel_id=1, source_target_pairs={{0,16},{1,17},{2,18},{3,19},{4,20},{5,21},{6,22},{7,23},{8,24},{9,... | collective-permute-start | bytes 3440648 | tf_op jit(solution)/shard_map/ppermute | solution.py:22
  445.6 82.2 %collective-permute-start.25 = (bf16[160,3584]{1,0:T(8,128)(2,1)S(1)}, bf16[160,3584]{1,0:T(8,128)(2,1)}, u32[]{:S(2)}, u32[]{:S(2)}) collective-permute-start(bf16[160,3584]{1,0:T(8,128)(2,1)S(1)} %bitcast.299), channel_id=1, source_target_pairs={{0,24},{1,25},{2,26},{3,27},{4,28},{5,29},{6,30},{7,31},{8,16},{9,... | collective-permute-start | bytes 3440648 | tf_op jit(solution)/shard_map/ppermute | solution.py:22
  539.2 41.3 %collective-permute-start.27 = (bf16[256,3584]{1,0:T(8,128)(2,1)S(1)}, bf16[256,3584]{1,0:T(8,128)(2,1)S(1)}, u32[]{:S(2)}, u32[]{:S(2)}) collective-permute-start(bf16[256,3584]{1,0:T(8,128)(2,1)S(1)} %fusion.34), channel_id=1, source_target_pairs={{0,2},{1,3},{2,0},{3,1},{4,6},{5,7},{6,4},{7,5},{8,10},{9,11},{10,... | collective-permute-start | bytes 5505032 | tf_op jit(solution)/shard_map/ppermute | solution.py:22
  540.5 40.0 %collective-permute-start.28 = (bf16[160,3584]{1,0:T(8,128)(2,1)S(1)}, bf16[160,3584]{1,0:T(8,128)(2,1)S(1)}, u32[]{:S(2)}, u32[]{:S(2)}) collective-permute-start(bf16[160,3584]{1,0:T(8,128)(2,1)S(1)} %bitcast.304), channel_id=1, source_target_pairs={{0,8},{1,9},{2,10},{3,11},{4,12},{5,13},{6,14},{7,15},{8,0},{9,1},... | collective-permute-start | bytes 3440648 | tf_op jit(solution)/shard_map/ppermute | solution.py:22
  540.7 39.7 %collective-permute-start.29 = (bf16[160,3584]{1,0:T(8,128)(2,1)S(1)}, bf16[160,3584]{1,0:T(8,128)(2,1)S(1)}, u32[]{:S(2)}, u32[]{:S(2)}) collective-permute-start(bf16[160,3584]{1,0:T(8,128)(2,1)S(1)} %bitcast.303), channel_id=1, source_target_pairs={{0,16},{1,17},{2,18},{3,19},{4,20},{5,21},{6,22},{7,23},{8,24},{9,... | collective-permute-start | bytes 3440648 | tf_op jit(solution)/shard_map/ppermute | solution.py:22
  541.9 50.2 %collective-permute-start.30 = (bf16[160,3584]{1,0:T(8,128)(2,1)S(1)}, bf16[160,3584]{1,0:T(8,128)(2,1)S(1)}, u32[]{:S(2)}, u32[]{:S(2)}) collective-permute-start(bf16[160,3584]{1,0:T(8,128)(2,1)S(1)} %bitcast.302), channel_id=1, source_target_pairs={{0,24},{1,25},{2,26},{3,27},{4,28},{5,29},{6,30},{7,31},{8,16},{9,... | collective-permute-start | bytes 3440648 | tf_op jit(solution)/shard_map/ppermute | solution.py:22
  601.5 80.6 %collective-permute-start.32 = (bf16[256,3584]{1,0:T(8,128)(2,1)S(1)}, bf16[256,3584]{1,0:T(8,128)(2,1)S(1)}, u32[]{:S(2)}, u32[]{:S(2)}) collective-permute-start(bf16[256,3584]{1,0:T(8,128)(2,1)S(1)} %fusion.33), channel_id=1, source_target_pairs={{0,6},{1,7},{2,4},{3,5},{4,2},{5,3},{6,0},{7,1},{8,14},{9,15},{10,... | collective-permute-start | bytes 5505032 | tf_op jit(solution)/shard_map/ppermute | solution.py:22
  602.6 79.5 %collective-permute-start.33 = (bf16[160,3584]{1,0:T(8,128)(2,1)S(1)}, bf16[160,3584]{1,0:T(8,128)(2,1)S(1)}, u32[]{:S(2)}, u32[]{:S(2)}) collective-permute-start(bf16[160,3584]{1,0:T(8,128)(2,1)S(1)} %bitcast.308), channel_id=1, source_target_pairs={{0,8},{1,9},{2,10},{3,11},{4,12},{5,13},{6,14},{7,15},{8,0},{9,1},... | collective-permute-start | bytes 3440648 | tf_op jit(solution)/shard_map/ppermute | solution.py:22
  602.8 79.3 %collective-permute-start.34 = (bf16[160,3584]{1,0:T(8,128)(2,1)S(1)}, bf16[160,3584]{1,0:T(8,128)(2,1)S(1)}, u32[]{:S(2)}, u32[]{:S(2)}) collective-permute-start(bf16[160,3584]{1,0:T(8,128)(2,1)S(1)} %bitcast.307), channel_id=1, source_target_pairs={{0,16},{1,17},{2,18},{3,19},{4,20},{5,21},{6,22},{7,23},{8,24},{9,... | collective-permute-start | bytes 3440648 | tf_op jit(solution)/shard_map/ppermute | solution.py:22
  604.0 78.1 %collective-permute-start.35 = (bf16[160,3584]{1,0:T(8,128)(2,1)S(1)}, bf16[160,3584]{1,0:T(8,128)(2,1)S(1)}, u32[]{:S(2)}, u32[]{:S(2)}) collective-permute-start(bf16[160,3584]{1,0:T(8,128)(2,1)S(1)} %bitcast.306), channel_id=1, source_target_pairs={{0,24},{1,25},{2,26},{3,27},{4,28},{5,29},{6,30},{7,31},{8,16},{9,... | collective-permute-start | bytes 3440648 | tf_op jit(solution)/shard_map/ppermute | solution.py:22
  690.8 78.7 %collective-permute-start.37 = (bf16[256,3584]{1,0:T(8,128)(2,1)S(1)}, bf16[256,3584]{1,0:T(8,128)(2,1)S(1)}, u32[]{:S(2)}, u32[]{:S(2)}) collective-permute-start(bf16[256,3584]{1,0:T(8,128)(2,1)S(1)} %fusion.32), channel_id=1, source_target_pairs={{0,4},{1,5},{2,6},{3,7},{4,0},{5,1},{6,2},{7,3},{8,12},{9,13},{10,... | collective-permute-start | bytes 5505032 | tf_op jit(solution)/shard_map/ppermute | solution.py:22
  (167 other events, 2933.2 us)
